TPU v7x, 32 devices: a whole 2x2x4 slice. The times are simulated.
32 devices in a mesh: gx: 4 (over y, x), gy: 8 (over z, core).
Axes of the slice: x: 2, y: 2, z: 4, core: 2. Of those that a mesh axis runs over, the one named last changes fastest.
Arguments:
- position: float32 [2, 24, 48, 128], P(None, 'gx', 'gy'), may hold values from 0 to 1
- velocity: float32 [2, 24, 48, 128], P(None, 'gx', 'gy'), may hold values from -3 to 3
- other_accel: float32 [2, 24, 48, 128], P(None, 'gx', 'gy'), may hold values from -5 to 5
- phase_ids: int32 [24, 48, 128], P('gx', 'gy'), may hold values from 0 to 1, as said below
- counts: int32 [24, 48], P('gx', 'gy'), may hold values from 48 to 128, as said below
Outputs:
- new_position: float32 [2, 24, 48, 128], P(None, 'gx', 'gy')
- new_velocity: float32 [2, 24, 48, 128], P(None, 'gx', 'gy')
- pressure: float32 [24, 48, 128], P('gx', 'gy')
- monitor: float32 [4, 4], replicated
Inputs may be any that keep to these rules, and one draw needn't show every extreme that they name: `counts`: each entry is the number of live slots of its cell; the live slots are the first ones of the cell; some cell holds 128. `phase_ids`: both phases occur among the live slots.
All inputs are finite; a program needn't handle non-finite values.
Results may differ from a plain program's by a relative error of at most 0.0001.
Values sent between devices are 32-bit elements; how exact they have to be, the bound alone decides.
A program may use at most 64 MiB of HBM per device.

v0:
```python
import functools

import jax
import jax.numpy as jnp
from jax import lax
from jax.experimental import pallas as pl
from jax.experimental.pallas import tpu as pltpu
from jax.sharding import PartitionSpec as P

ITERS = 4


TIME_STEP = 0.05
KERNEL_NORM = 4.0 / (3.141592653589793 * 64.0)
REST_LIGHT = 1.2
REST_HEAVY = 1.5
STIFF_LIGHT = 100.0
STIFF_HEAVY = 200.0
MASS_LIGHT = 1.0
MASS_HEAVY = 1.5
SENTINEL = 1e30


EMPTY = -1e30
FAR = 1e30
LIMIT = 1e29
DIRS = tuple((dx, dy) for dx in (-1, 0, 1) for dy in (-1, 0, 1) if dx or dy)


def split3(value):
    high = value.astype(jnp.bfloat16).astype(jnp.float32)
    rest = value - high
    mid = rest.astype(jnp.bfloat16).astype(jnp.float32)
    low = (rest - mid).astype(jnp.bfloat16).astype(jnp.float32)
    return high, mid, low


def put_rows(ref, row, values, width):
    for at, value in enumerate(values):
        ref[row, at * width : (at + 1) * width, :] = value


def source_features(x, y, live, jf, row, width):
    x = jnp.where(live, x - 0.5, 0.0)
    y = jnp.where(live, y - 0.5, 0.0)
    xh, xm, xl = split3(x)
    yh, ym, yl = split3(y)
    bh, bm, bl = split3(jnp.where(live, -(x * x + y * y), EMPTY))
    one = jnp.ones_like(x)
    nil = jnp.zeros_like(x)
    put_rows(
        jf,
        row,
        [xh, xh, xm, xh, xl, xm, bh, bm, yh, yh, ym, yh, yl, ym, bl, nil]
        + [one, one, one, nil, nil, nil, nil, nil],
        width,
    )


def pair_features(jf, lhs, row, width, half):
    for n in range(width - half):
        first = jf[row, pl.ds(n, 24, stride=width), :]
        second = jf[row, pl.ds(n + half, 24, stride=width), :]
        both = jnp.concatenate([first, second], axis=0)
        lhs[row, n] = both.T.astype(jnp.bfloat16)


def target_features(x, y, xf, yf, af, row, width):
    x = jnp.where(x < LIMIT, x, 0.0) - 0.5
    y = y - 0.5
    one = jnp.ones_like(x)
    nil = jnp.zeros_like(x)
    for at in range(3):
        h, m, l = split3(2.0 * (x - (at - 1.0)))
        put_rows(xf.at[row], at, [h, m, h, l, h, m, one, one], width)
        h, m, l = split3(2.0 * (y - (at - 1.0)))
        put_rows(yf.at[row], at, [h, m, h, l, h, m, one, nil], width)
    for ax in range(3):
        for ay in range(3):
            dx = x - (ax - 1.0)
            dy = y - (ay - 1.0)
            h, m, l = split3(1.0 - (dx * dx + dy * dy))
            put_rows(af.at[row], 3 * ax + ay, [h, m, l, nil, nil, nil, nil, nil], width)


def target_block(xf, yf, af, row, cell, ax, ay, width):
    return jnp.concatenate(
        [
            xf[row, ax, pl.ds(cell + 1, 8, stride=width), :],
            yf[row, ay, pl.ds(cell + 1, 8, stride=width), :],
            af[row, 3 * ax + ay, pl.ds(cell + 1, 8, stride=width), :],
        ],
        axis=0,
    )


def overlap(lhs, xf, yf, af, row, cell, ax, ay, width, half):
    first = target_block(xf, yf, af, row, cell, ax, ay, width)
    second = target_block(xf, yf, af, row, cell + half, ax, ay, width)
    nil = jnp.zeros_like(first)
    rhs = jnp.concatenate(
        [
            jnp.concatenate([first, nil], axis=1),
            jnp.concatenate([nil, second], axis=1),
        ],
        axis=0,
    ).astype(jnp.bfloat16)
    raw = jnp.dot(lhs[row + ax, cell + ay], rhs, preferred_element_type=jnp.float32)
    return jnp.maximum(raw, 0.0)


def all_features(pos, jf, lhs, xf, yf, af, rows, width, half):
    def source_row(row, carry):
        source_features(pos[0, row], pos[1, row], pos[0, row] < LIMIT, jf, row, width)
        pair_features(jf, lhs, row, width, half)
        return carry

    lax.fori_loop(0, rows + 2, source_row, 0)

    def target_row(row, carry):
        target_features(pos[0, row + 1], pos[1, row + 1], xf, yf, af, row, width)
        return carry

    lax.fori_loop(0, rows, target_row, 0)


def value_rows(x, y, term, live, vf, row, width):
    x = jnp.where(live, x - 0.5, 0.0)
    y = jnp.where(live, y - 0.5, 0.0)
    term = jnp.where(live, term, 0.0)
    highs, mids = [], []
    for value in (jnp.ones_like(x), x, y, term, term * x, term * y):
        high, mid, _ = split3(value)
        highs.append(high)
        mids.append(mid)
    nil = jnp.zeros_like(x)
    put_rows(vf, row, highs + [nil, nil] + mids + [nil, nil], width)


def density_row(lhs, xf, yf, af, dens, ghi, glo, row, cols, slots):
    width, half = cols + 2, cols // 2
    for cell in range(half):
        total = jnp.zeros((8, 2 * slots), jnp.float32)
        for ax in range(3):
            for ay in range(3):
                w = overlap(lhs, xf, yf, af, row, cell, ax, ay, width, half)
                square = w * w
                high = square.astype(jnp.bfloat16)
                ghi[row, cell, 3 * ax + ay] = high
                glo[row, cell, 3 * ax + ay] = (square - high.astype(jnp.float32)).astype(
                    jnp.bfloat16
                )
                total = total + jnp.sum(
                    (square * w).reshape(slots // 8, 8, 2 * slots), axis=0
                )
        got = jnp.sum(total, axis=0, keepdims=True)
        dens[row, cell + 1 : cell + 2, :] = got[:, :slots]
        dens[row, cell + half + 1 : cell + half + 2, :] = got[:, slots:]


def force_row(vf, ghi, glo, sums, row, cols, slots):
    width, half = cols + 2, cols // 2
    for cell in range(half):
        zero = jnp.zeros((8, slots), jnp.float32)
        parts = [[zero, zero, zero], [zero, zero, zero]]
        for ax in range(3):
            for ay in range(3):
                value = jnp.concatenate(
                    [
                        vf[row + ax, pl.ds(cell + ay, 16, stride=width), :],
                        vf[row + ax, pl.ds(cell + ay + half, 16, stride=width), :],
                    ],
                    axis=0,
                ).astype(jnp.bfloat16)
                got = jnp.dot(
                    value, ghi[row, cell, 3 * ax + ay], preferred_element_type=jnp.float32
                ) + jnp.dot(
                    value, glo[row, cell, 3 * ax + ay], preferred_element_type=jnp.float32
                )
                pieces = (
                    got[0:8, :slots] + got[8:16, :slots],
                    got[16:24, slots:] + got[24:32, slots:],
                )
                for acc, piece in zip(parts, pieces):
                    acc[0] = acc[0] + piece
                    if ax != 1:
                        acc[1] = acc[1] + piece if ax == 2 else acc[1] - piece
                    if ay != 1:
                        acc[2] = acc[2] + piece if ay == 2 else acc[2] - piece
        for at, acc in zip((cell, cell + half), parts):
            plain, by_x, by_y = acc
            rows_out = (
                plain[0:1],
                plain[1:2] + by_x[0:1],
                plain[2:3] + by_y[0:1],
                plain[3:4],
                plain[4:5] + by_x[3:4],
                plain[5:6] + by_y[3:4],
            )
            for k, value in enumerate(rows_out):
                sums[k, at + 1 : at + 2, :] = value


def remote(src, dst, send, recv, to_x, to_y):
    return pltpu.make_async_remote_copy(
        src_ref=src,
        dst_ref=dst,
        send_sem=send,
        recv_sem=recv,
        device_id=(to_x, to_y),
        device_id_type=pl.DeviceIdType.MESH,
    )


def pack_edges(field, out, par, count, rows, cols):
    for d, (dx, dy) in enumerate(DIRS):
        row = rows if dx > 0 else 1
        cell = cols if dy > 0 else 1
        for k in range(count):
            if dy == 0:
                out[par, d, k, : cols + 2, :] = field[k, row]
            elif dx == 0:
                for r in range(1, rows + 1):
                    out[par, d, k, r : r + 1, :] = field[k, r, cell : cell + 1, :]
            else:
                out[par, d, k, 0:1, :] = field[k, row, cell : cell + 1, :]


def unpack_edges(field, got, par, count, rows, cols):
    for d, (dx, dy) in enumerate(DIRS):
        row = 0 if dx > 0 else rows + 1
        cell = 0 if dy > 0 else cols + 1
        for k in range(count):
            if dy == 0:
                field[k, row, 1 : cols + 1, :] = got[par, d, k, 1 : cols + 1, :]
            elif dx == 0:
                for r in range(1, rows + 1):
                    field[k, r, cell : cell + 1, :] = got[par, d, k, r : r + 1, :]
            else:
                field[k, row, cell : cell + 1, :] = got[par, d, k, 0:1, :]


def step_kernel(
    nx, ny,
    pos_in, vel_in, oth_in, code_in,
    pos_out, vel_out, press_out, bounds_out,
    base, pos, acc, press, parts, ratio, dens,
    jf, lhs, xf, yf, af, vf, sums, ghi, glo,
    pos_snd, pos_rcv, ab_snd, ab_rcv, one_snd, one_rcv, two_snd, two_rcv,
    pos_ss, pos_rs, ab_ss, ab_rs, one_ss, one_rs, two_ss, two_rs,
):
    _, rows, cols, slots = pos_in.shape
    width, half = cols + 2, cols // 2
    me_x, me_y = lax.axis_index("gx"), lax.axis_index("gy")

    def at_x(step):
        return lax.rem(me_x + step + nx, nx)

    def at_y(step):
        return lax.rem(me_y + step + ny, ny)

    barrier = pltpu.get_barrier_semaphore()
    partners = [(0, k) for k in range(1, ny)] + [(k, 0) for k in range(1, nx)]
    partners += [(dx, dy) for dx, dy in DIRS if dx and dy]
    for dx, dy in partners:
        pl.semaphore_signal(
            barrier, inc=1, device_id=(at_x(dx), at_y(dy)), device_id_type=pl.DeviceIdType.MESH
        )

    for ref in (base, acc, press, ratio, dens, sums, parts, pos):
        ref[...] = jnp.zeros_like(ref)
    for ref in (pos_snd, ab_snd):
        ref[...] = jnp.zeros_like(ref)
    for row in range(rows):
        for k, source in enumerate((pos_in, vel_in, oth_in)):
            for c in range(2):
                base[2 * k + c, row, 1 : cols + 1, :] = source[c, row]
        base[6, row, 1 : cols + 1, :] = code_in[row]
    pl.semaphore_wait(barrier, len(partners))

    def halo(src, dst, send, recv, par):
        return [
            remote(src.at[par, d], dst.at[par, d], send.at[par, d], recv.at[par, d], at_x(dx), at_y(dy))
            for d, (dx, dy) in enumerate(DIRS)
        ]

    def one_iteration(it, carry):
        par = lax.rem(it, 2)

        def predict(row, carry):
            live = base[6, row] > 0
            for c in range(2):
                vel = base[2 + c, row] + TIME_STEP * (base[4 + c, row] + acc[c, row])
                moved = base[c, row] + TIME_STEP * vel
                pos[c, row + 1] = jnp.where(live, moved, FAR if c == 0 else 0.0)
            return carry

        lax.fori_loop(0, rows, predict, 0)
        pack_edges(pos, pos_snd, par, 2, rows, cols)
        copies = halo(pos_snd, pos_rcv, pos_ss, pos_rs, par)
        for copy in copies:
            copy.start()
        for copy in copies:
            copy.wait()
        unpack_edges(pos, pos_rcv, par, 2, rows, cols)

        all_features(pos, jf, lhs, xf, yf, af, rows, width, half)

        def density_step(row, carry):
            density_row(lhs, xf, yf, af, dens, ghi, glo, row, cols, slots)
            return carry

        lax.fori_loop(0, rows, density_step, 0)

        def bounds_step(row, carry):
            code = base[6, row]
            live = code > 0.5
            heavy = code > 1.5
            density = KERNEL_NORM * dens[row]
            own = density / jnp.where(heavy, REST_HEAVY, REST_LIGHT)
            ratio[row] = own
            safe = jnp.where(live, density, 1.0)
            alpha = jnp.where(live, press[row] / (safe * safe), 0.0)
            stiff = jnp.where(heavy, STIFF_HEAVY, STIFF_LIGHT)
            beta = jnp.where(live, stiff * (own - 1.0) / (safe * safe), 0.0)
            parts[0, row + 1] = alpha
            parts[1, row + 1] = jnp.where(heavy, 0.0, beta)
            parts[2, row + 1] = jnp.where(heavy, beta, 0.0)
            light_sel = live & jnp.logical_not(heavy)
            heavy_sel = live & heavy
            return (
                jnp.maximum(carry[0], jnp.where(light_sel, own, -SENTINEL)),
                jnp.maximum(carry[1], jnp.where(heavy_sel, own, -SENTINEL)),
                jnp.maximum(carry[2], jnp.where(light_sel, -own, -SENTINEL)),
                jnp.maximum(carry[3], jnp.where(heavy_sel, -own, -SENTINEL)),
            )

        floor = jnp.full((width, slots), -SENTINEL, jnp.float32)
        local = lax.fori_loop(0, rows, bounds_step, (floor,) * 4)
        for k, value in enumerate(local):
            one_snd[par, k : k + 1, :] = jnp.max(value, axis=0, keepdims=True)
        one_snd[par, 4:8, :] = jnp.full((4, slots), -SENTINEL, jnp.float32)
        firsts = [
            remote(one_snd.at[par], one_rcv.at[par, k], one_ss.at[par, k], one_rs.at[par, k], me_x, at_y(k))
            for k in range(1, ny)
        ]
        for copy in firsts:
            copy.start()
        pack_edges(parts, ab_snd, par, 3, rows, cols)
        copies = halo(ab_snd, ab_rcv, ab_ss, ab_rs, par)
        for copy in copies:
            copy.start()
        for copy in firsts:
            copy.wait()
        best = one_snd[par]
        for k in range(1, ny):
            best = jnp.maximum(best, one_rcv[par, k])
        two_snd[par] = best
        seconds = [
            remote(two_snd.at[par], two_rcv.at[par, k], two_ss.at[par, k], two_rs.at[par, k], at_x(k), me_y)
            for k in range(1, nx)
        ]
        for copy in seconds:
            copy.start()
        for copy in copies:
            copy.wait()
        unpack_edges(parts, ab_rcv, par, 3, rows, cols)
        for copy in seconds:
            copy.wait()
        for k in range(1, nx):
            best = jnp.maximum(best, two_rcv[par, k])
        bound = jnp.max(best, axis=1, keepdims=True)
        bounds_out[it] = jnp.broadcast_to(bound, (8, slots))
        relax = 1.0 / (1.0 + bound[0:2] + bound[2:4])
        relax_light = relax[0:1]
        relax_heavy = relax[1:2]

        def term_step(row, carry):
            term = parts[0, row] + relax_light * parts[1, row] + relax_heavy * parts[2, row]
            value_rows(pos[0, row], pos[1, row], term, pos[0, row] < LIMIT, vf, row, width)
            return carry

        lax.fori_loop(0, rows + 2, term_step, 0)

        def force_step(row, carry):
            force_row(vf, ghi, glo, sums, row, cols, slots)
            code = base[6, row]
            live = code > 0.5
            heavy = code > 1.5
            relaxed = jnp.where(heavy, STIFF_HEAVY * relax_heavy, STIFF_LIGHT * relax_light)
            press[row] = jnp.where(live, press[row] + relaxed * (ratio[row] - 1.0), 0.0)
            term = (
                parts[0, row + 1]
                + relax_light * parts[1, row + 1]
                + relax_heavy * parts[2, row + 1]
            )
            scale = jnp.where(
                heavy, 6.0 * KERNEL_NORM / MASS_HEAVY, 6.0 * KERNEL_NORM / MASS_LIGHT
            )
            for c in range(2):
                own = pos[c, row + 1] - 0.5
                force = term * (own * sums[0] - sums[1 + c]) + own * sums[3] - sums[4 + c]
                acc[c, row] = jnp.where(live, scale * force, 0.0)
            return carry

        lax.fori_loop(0, rows, force_step, 0)
        return carry

    lax.fori_loop(0, ITERS, one_iteration, 0)

    def finish(row, carry):
        live = base[6, row] > 0.5
        press_out[row] = press[row, 1 : cols + 1, :]
        for c in range(2):
            vel = base[2 + c, row] + TIME_STEP * (base[4 + c, row] + acc[c, row])
            vel = jnp.where(live, vel, 0.0)
            place = jnp.where(live, base[c, row] + TIME_STEP * vel, 0.0)
            vel_out[c, row] = vel[1 : cols + 1]
            pos_out[c, row] = place[1 : cols + 1]
        return carry

    lax.fori_loop(0, rows, finish, 0)


def local(position, velocity, other_accel, phase_ids, counts):
    rows, cols, slots = phase_ids.shape
    width, half = cols + 2, cols // 2
    nx, ny = lax.axis_size("gx"), lax.axis_size("gy")
    high = max(width, rows + 2)
    slot_index = jnp.arange(slots, dtype=jnp.int32)
    live = slot_index[None, None, :] < counts[:, :, None]
    codes = jnp.where(live, phase_ids + 1, 0).astype(jnp.float32)

    def vm(*shape):
        return pltpu.VMEM(shape, jnp.float32)

    def half_vm(*shape):
        return pltpu.VMEM(shape, jnp.bfloat16)

    dma = pltpu.SemaphoreType.DMA
    new_pos, new_vel, pressure, bounds = pl.pallas_call(
        functools.partial(step_kernel, nx, ny),
        out_shape=(
            jax.ShapeDtypeStruct((2, rows, cols, slots), jnp.float32),
            jax.ShapeDtypeStruct((2, rows, cols, slots), jnp.float32),
            jax.ShapeDtypeStruct((rows, cols, slots), jnp.float32),
            jax.ShapeDtypeStruct((ITERS, 8, slots), jnp.float32),
        ),
        in_specs=[pl.BlockSpec(memory_space=pltpu.VMEM)] * 4,
        out_specs=(pl.BlockSpec(memory_space=pltpu.VMEM),) * 4,
        scratch_shapes=[
            vm(7, rows, width, slots),
            vm(2, rows + 2, width, slots),
            vm(2, rows, width, slots),
            vm(rows, width, slots),
            vm(3, rows + 2, width, slots),
            vm(rows, width, slots),
            vm(rows, width, slots),
            vm(rows + 2, 24 * width, slots),
            half_vm(rows + 2, width - half, slots, 48),
            vm(rows, 3, 8 * width, slots),
            vm(rows, 3, 8 * width, slots),
            vm(rows, 9, 8 * width, slots),
            vm(rows + 2, 16 * width, slots),
            vm(6, width, slots),
            half_vm(rows, half, 9, slots, 2 * slots),
            half_vm(rows, half, 9, slots, 2 * slots),
            vm(2, 8, 2, high, slots),
            vm(2, 8, 2, high, slots),
            vm(2, 8, 3, high, slots),
            vm(2, 8, 3, high, slots),
            vm(2, 8, slots),
            vm(2, ny, 8, slots),
            vm(2, 8, slots),
            vm(2, nx, 8, slots),
            dma((2, 8)), dma((2, 8)), dma((2, 8)), dma((2, 8)),
            dma((2, ny)), dma((2, ny)), dma((2, nx)), dma((2, nx)),
        ],
        compiler_params=pltpu.CompilerParams(collective_id=0, has_side_effects=True),
    )(position, velocity, other_accel, codes)
    tops = bounds[:, :2, 0]
    lows = -bounds[:, 2:4, 0]
    return new_pos, new_vel, pressure, jnp.concatenate([tops, lows], axis=1)


def solution(mesh):
    placed = (
        P(None, "gx", "gy", None),
        P(None, "gx", "gy", None),
        P(None, "gx", "gy", None),
        P("gx", "gy", None),
        P("gx", "gy"),
    )
    return jax.shard_map(
        local,
        mesh=mesh,
        in_specs=placed,
        out_specs=(P(None, "gx", "gy", None), P(None, "gx", "gy", None), P("gx", "gy", None), P()),
        check_vma=False,
    )
```

profile of v0, /device:TPU:0, one launch (start us, length us, event | category | flops | bytes accessed | tf_op | source)
XLA Modules:
  0.0 109.3 jit_solution(10360887232802700601)
XLA Ops:
  0.6 0.0 copy-start.1
  0.6 1.4 %select_convert_fusion.code_in = f32[6,6,128]{2,1,0:T(8,128)} fusion(s32[6,6,128]{2,1,0:T(8,128)} %param.8, s32[6,6]{1,0:T(8,128)} %param.9), kind=kLoop, calls=%fused_computation | loop fusion | flops 18432 | bytes 37008 | tf_op jit(solution)/shard_map/convert_element_type | solution.py:432
  2.1 0.0 copy-done.1
  2.1 0.0 copy-start.2
  2.1 0.6 copy.17.pos_in
  2.7 0.1 copy-done.2
  2.8 0.0 copy-start.3
  2.8 0.6 copy.18.vel_in
  3.5 0.1 copy-done.3
  3.6 0.6 copy.19.oth_in
  4.2 101.3 %shard_map.84 = (f32[2,6,6,128]{3,2,1,0:T(8,128)}, f32[2,6,6,128]{3,2,1,0:T(8,128)}, f32[6,6,128]{2,1,0:T(8,128)}, f32[4,8,128]{2,1,0:T(8,128)}) custom-call(f32[2,6,6,128]{3,2,1,0:T(8,128)} %copy.17.pos_in, f32[2,6,6,128]{3,2,1,0:T(8,128)} %copy.18.vel_in, f32[2,6,6,128]{3,2,1,0:T(8,128)} %copy.19.oth_in, f32[6,6,128]{2,1,0:T(8,128)} %select_convert_fusion.code_in), custom_call_target="tpu_custom_call" | custom-call | tf_op jit(solution)/shard_map/pallas_call | solution.py:441
  105.6 0.0 copy-start.5
  105.6 0.0 copy-start
  105.6 1.5 %copy.22 = f32[2,6,6,128]{3,0,2,1:T(2,128)} copy(f32[2,6,6,128]{3,2,1,0:T(8,128)} %get-tuple-element.16) | data formatting | bytes 73728
  107.1 0.0 copy-done.5
  107.1 0.1 copy.20
  107.2 0.1 copy.21
  107.3 0.7 copy.24
  107.9 0.0 copy-done
  108.0 0.0 copy-start.4
  108.0 0.6 copy.23
  108.6 0.1 copy-done.4
  108.7 0.6 copy.26
  (2 shorter events, 0.0 us)
Async XLA Ops:
  0.6 1.4 %copy-start.1 = (f32[2,6,6,128]{3,0,2,1:T(2,128)S(1)}, f32[2,6,6,128]{3,0,2,1:T(2,128)}, u32[]{:S(2)}) copy-start(f32[2,6,6,128]{3,0,2,1:T(2,128)} %param.5) | copy-start | bytes 110596
  2.1 0.8 copy-start.2
  2.8 0.8 copy-start.3
  105.6 1.5 %copy-start.5 = (f32[4,8,128]{2,1,0:T(8,128)S(1)}, f32[4,8,128]{2,1,0:T(8,128)}, u32[]{:S(2)}) copy-start(f32[4,8,128]{2,1,0:T(8,128)} %get-tuple-element.11) | copy-start | bytes 49156
  105.6 2.4 %copy-start = (f32[2,6,6,128]{3,2,1,0:T(8,128)S(1)}, f32[2,6,6,128]{3,2,1,0:T(8,128)}, u32[]{:S(2)}) copy-start(f32[2,6,6,128]{3,2,1,0:T(8,128)} %get-tuple-element.17) | copy-start | bytes 110596
  108.0 0.7 copy-start.4
where the time goes:
time: 110 us; the launch traced here: 109 us
  Pallas kernels  101 us (92%)
  local copies, waits for them, and re-layouts  5.84 us (5%)
  other arithmetic  1.44 us (1%)
    pallas_call x1, Pallas kernels, local(): pl.pallas_call(functools.partial(step_kernel, nx, ny), out_shape=(jax.Sha...  101 us
    unnamed x19, local copies, waits for them, and re-layouts  5.64 us

commit v1 on v0

v1 whole, which is shorter than its diff:
```python
import functools

import jax
import jax.numpy as jnp
from jax import lax
from jax.experimental import pallas as pl
from jax.experimental.pallas import tpu as pltpu
from jax.sharding import PartitionSpec as P

ITERS = 4


TIME_STEP = 0.05
KERNEL_NORM = 4.0 / (3.141592653589793 * 64.0)
REST_LIGHT = 1.2
REST_HEAVY = 1.5
STIFF_LIGHT = 100.0
STIFF_HEAVY = 200.0
MASS_LIGHT = 1.0
MASS_HEAVY = 1.5
SENTINEL = 1e30


EMPTY = -1e30
FAR = 1e30
LIMIT = 1e29
DIAGONALS = tuple((dx, dy) for dx in (-1, 1) for dy in (-1, 1))
SIDES = ((-1, 0), (1, 0), (0, -1), (0, 1))
DIRS = DIAGONALS + SIDES


def rounded(value):
    return value.astype(jnp.bfloat16).astype(jnp.float32)


def split2(value):
    high = rounded(value)
    return high, rounded(value - high)


def split3(value):
    high = rounded(value)
    rest = value - high
    mid = rounded(rest)
    return high, mid, rounded(rest - mid)


def put_rows(ref, at, values, width):
    for k, value in enumerate(values):
        ref[at, k * width : (k + 1) * width, :] = value


def source_features(x, y, ref, at, width):
    live = x < LIMIT
    x = jnp.where(live, x - 0.5, 0.0)
    y = jnp.where(live, y - 0.5, 0.0)
    xh, xm, xl = split3(x)
    yh, ym, yl = split3(y)
    bh, bm, bl = split3(jnp.where(live, -(x * x + y * y), EMPTY))
    put_rows(
        ref,
        at,
        [xh, xh, xm, xh, xl, xm, bh, bm, yh, yh, ym, yh, yl, ym, bl],
        width,
    )


def source_constants(ref, at, width, like):
    nil, one = jnp.zeros_like(like), jnp.ones_like(like)
    for k in range(15, 24):
        ref[at, k * width : (k + 1) * width, :] = one if 16 <= k <= 18 else nil


def target_features(x, y, xf, yf, af, row, width):
    x = jnp.where(x < LIMIT, x, 0.0) - 0.5
    y = y - 0.5
    for at in range(3):
        h, m, l = split3(2.0 * (x - (at - 1.0)))
        put_rows(xf.at[row], at, [h, m, h, l, h, m], width)
        h, m, l = split3(2.0 * (y - (at - 1.0)))
        put_rows(yf.at[row], at, [h, m, h, l, h, m], width)
    for ax in range(3):
        for ay in range(3):
            dx = x - (ax - 1.0)
            dy = y - (ay - 1.0)
            put_rows(af.at[row], 3 * ax + ay, split3(1.0 - (dx * dx + dy * dy)), width)


def target_constants(xf, yf, af, row, width, like):
    nil, one = jnp.zeros_like(like), jnp.ones_like(like)
    for at in range(3):
        for ref, values in ((xf, (one, one)), (yf, (one, nil))):
            for k, value in enumerate(values):
                ref[row, at, (6 + k) * width : (7 + k) * width, :] = value
    for at in range(9):
        for k in range(3, 8):
            af[row, at, k * width : (k + 1) * width, :] = nil


def value_rows(x, y, parts, ref, at, width):
    live = x < LIMIT
    x = jnp.where(live, x - 0.5, 0.0)
    y = jnp.where(live, y - 0.5, 0.0)
    parts = [jnp.where(live, part, 0.0) for part in parts]
    splits = [split2(part) for part in parts]
    one = jnp.where(live, 1.0, 0.0)
    nil = jnp.zeros_like(x)
    groups = [[one] + [h for h, _ in splits] + [m for _, m in splits] + [nil]]
    for coord in (x, y):
        for shift in (-1.0, 0.0, 1.0):
            moved = jnp.where(live, coord + shift, 0.0)
            splits = [split2(moved)] + [split2(part * moved) for part in parts]
            groups.append([h for h, _ in splits] + [m for _, m in splits])
    put_rows(ref, at, [row for group in groups for row in group], width)


def remote(src, dst, send, recv, to_x, to_y):
    return pltpu.make_async_remote_copy(
        src_ref=src,
        dst_ref=dst,
        send_sem=send,
        recv_sem=recv,
        device_id=(to_x, to_y),
        device_id_type=pl.DeviceIdType.MESH,
    )


def step_kernel(
    nx, ny,
    pos_in, vel_in, oth_in, code_in,
    pos_out, vel_out, press_out, bounds_out,
    base, pos, acc, press, parts, ratio, dens, dsum,
    jf, jfh, lhs, xf, yf, af, vf, vfh, sums, gram,
    pos_pack, pos_row, pos_col, pos_cor, ab_pack, ab_row, ab_col, ab_cor,
    red_snd, red_rcv,
    pos_ss, pos_rs, ab_ss, ab_rs, red_ss, red_rs,
):
    _, rows, cols, slots = pos_in.shape
    width, half = cols + 2, cols // 2
    others = nx * ny - 1
    me_x, me_y = lax.axis_index("gx"), lax.axis_index("gy")

    def at_x(step):
        return lax.rem(me_x + step + nx, nx)

    def at_y(step):
        return lax.rem(me_y + step + ny, ny)

    for ref in (pos_row, pos_col, pos_cor, ab_row, ab_col, ab_cor):
        ref[...] = jnp.zeros_like(ref)
    peers = [(dx, dy) for dx in range(nx) for dy in range(ny) if dx or dy]
    barrier = pltpu.get_barrier_semaphore()
    for dx, dy in peers:
        pl.semaphore_signal(
            barrier, inc=1, device_id=(at_x(dx), at_y(dy)), device_id_type=pl.DeviceIdType.MESH
        )

    for ref in (base, acc, press, pos, dens, ratio, parts, sums, pos_pack, ab_pack):
        ref[...] = jnp.zeros_like(ref)
    like = jnp.zeros((width, slots), jnp.float32)
    for row in range(rows):
        for k, source in enumerate((pos_in, vel_in, oth_in)):
            for c in range(2):
                base[2 * k + c, row, 1 : cols + 1, :] = source[c, row]
        base[6, row, 1 : cols + 1, :] = code_in[row]
        target_constants(xf, yf, af, row, width, like)
    for row in range(rows + 2):
        source_constants(jf, row, width, like)
    for at in range(3):
        source_constants(jfh, at, 8, jnp.zeros((8, slots), jnp.float32))
    pl.semaphore_wait(barrier, others)

    def halo(field, pack, row_got, col_got, cor_got, send, recv, par):
        copies = []
        for d, (dx, dy) in enumerate(DIRS):
            row = rows - 1 if dx > 0 else 0
            side_x, side_y = (0 if dx > 0 else 1), (0 if dy > 0 else 1)
            if dy == 0:
                src, dst = field.at[:, row], row_got.at[par, side_x]
            elif dx == 0:
                src = pack.at[1 - side_y, :, pl.ds(0, rows)]
                dst = col_got.at[par, side_y, :, pl.ds(0, rows)]
            else:
                src = pack.at[1 - side_y, :, pl.ds(row, 1)]
                dst = cor_got.at[par, :, pl.ds(2 * side_x + side_y, 1)]
            copies.append(remote(src, dst, send.at[par, d], recv.at[par, d], at_x(dx), at_y(dy)))
        return copies

    def pack_columns(field, pack, count):
        for k in range(count):
            for side, cell in enumerate((1, cols)):
                for r in range(rows):
                    pack[side, k, r : r + 1, :] = field[k, r, cell : cell + 1, :]

    def cell_rows(inner, outer, srow, col, pick):
        if 1 <= col <= cols:
            return inner[srow, pick(col, width), :]
        side = 0 if col == 0 else 1
        if srow in (0, rows + 1):
            return outer[2, pick(2 * (0 if srow == 0 else 1) + side, 8), :]
        return outer[side, pick(srow - 1, 8), :]

    def build_lhs(srow, q):
        def pick(at, step):
            return pl.ds(at, 24, stride=step)

        both = jnp.concatenate(
            [
                cell_rows(jf, jfh, srow, q, pick),
                cell_rows(jf, jfh, srow, width - 1 - q, pick),
            ],
            axis=0,
        )
        lhs[srow, q] = both.T.astype(jnp.bfloat16)

    def target_block(row, cell, ax, ay):
        at = pl.ds(cell, 8, stride=width)
        return jnp.concatenate(
            [xf[row, ax, at, :], yf[row, ay, at, :], af[row, 3 * ax + ay, at, :]], axis=0
        )

    def density_block(row, p, ax, ay):
        first = target_block(row, p + 1, ax, ay)
        second = target_block(row, cols - p, ax, 2 - ay)
        nil = jnp.zeros_like(first)
        rhs = jnp.concatenate(
            [
                jnp.concatenate([first, nil], axis=1),
                jnp.concatenate([nil, second], axis=1),
            ],
            axis=0,
        ).astype(jnp.bfloat16)
        raw = jnp.dot(lhs[row + ax, p + ay], rhs, preferred_element_type=jnp.float32)
        w = jnp.maximum(raw, 0.0)
        square = w * w
        gram[row, p, 3 * ax + ay] = square
        return jnp.sum((square * w).reshape(slots // 8, 8, 2 * slots), axis=0)

    def density_blocks(row, p, blocks, fresh):
        total = None if fresh else dsum[row, p]
        for ax, ay in blocks:
            got = density_block(row, p, ax, ay)
            total = got if total is None else total + got
        dsum[row, p] = total

    def value_cell(srow, col, ax, ay):
        def pick(group):
            return lambda at, step: pl.ds(8 * step * group + at, 8, stride=step)

        return [
            cell_rows(vf, vfh, srow, col, pick(group)) for group in (0, 1 + ax, 4 + ay)
        ]

    def force_blocks(row, p, blocks, fresh):
        left, high, low = [], [], []
        for ax, ay in blocks:
            q = p + ay
            left.append(
                jnp.concatenate(
                    value_cell(row + ax, q, ax, ay)
                    + value_cell(row + ax, width - 1 - q, ax, 2 - ay),
                    axis=0,
                ).astype(jnp.bfloat16)
            )
            g = gram[row, p, 3 * ax + ay]
            h = g.astype(jnp.bfloat16)
            high.append(h)
            low.append((g - h.astype(jnp.float32)).astype(jnp.bfloat16))
        got = jnp.dot(
            jnp.concatenate(left + left, axis=1),
            jnp.concatenate(high + low, axis=0),
            preferred_element_type=jnp.float32,
        )
        for col, piece in ((p + 1, got[:24, :slots]), (cols - p, got[24:, slots:])):
            at = pl.ds(col, 24, stride=width)
            sums[row, at, :] = piece if fresh else sums[row, at, :] + piece

    every = [(ax, ay) for ax in range(3) for ay in range(3)]

    def inner_blocks(row, p):
        return [
            (ax, ay)
            for ax, ay in every
            if 1 <= row + ax <= rows and 1 <= p + ay <= cols
        ]

    def inner_phase(blocks_of):
        def middle(step, carry):
            for k in range(2):
                for p in range(half):
                    blocks_of(1 + 2 * step + k, p, inner_blocks(1, p), True)
            return carry

        pairs = (rows - 2) // 2
        lax.fori_loop(0, pairs, middle, 0)
        for row in [0] + list(range(1 + 2 * pairs, rows)):
            for p in range(half):
                blocks_of(row, p, inner_blocks(row, p), True)

    def outer_phase(blocks_of, corners):
        for row in range(rows):
            for p in range(half):
                inner = inner_blocks(row, p)
                blocks = [
                    (ax, ay)
                    for ax, ay in every
                    if (ax, ay) not in inner
                    and (row + ax in (0, rows + 1) and p + ay == 0) == corners
                ]
                if blocks:
                    blocks_of(row, p, blocks, False)

    def one_iteration(it, carry):
        par = lax.rem(it, 2)

        for row in range(rows):
            live = base[6, row] > 0
            for c in range(2):
                vel = base[2 + c, row] + TIME_STEP * (base[4 + c, row] + acc[c, row])
                moved = base[c, row] + TIME_STEP * vel
                pos[c, row] = jnp.where(live, moved, FAR if c == 0 else 0.0)
        pack_columns(pos, pos_pack, 2)
        pos_copies = halo(pos, pos_pack, pos_row, pos_col, pos_cor, pos_ss, pos_rs, par)
        for copy in pos_copies:
            copy.start()

        for row in range(rows):
            source_features(pos[0, row], pos[1, row], jf, row + 1, width)
            for q in range(1, half + 2):
                build_lhs(row + 1, q)
        for row in range(rows):
            target_features(pos[0, row], pos[1, row], xf, yf, af, row, width)
        inner_phase(density_blocks)

        for copy in pos_copies[4:]:
            copy.wait_recv()
        for side, srow in enumerate((0, rows + 1)):
            source_features(pos_row[par, side, 0], pos_row[par, side, 1], jf, srow, width)
            source_features(pos_col[par, side, 0], pos_col[par, side, 1], jfh, side, 8)
            for q in range(1, half + 2):
                build_lhs(srow, q)
        for row in range(rows):
            build_lhs(row + 1, 0)
        outer_phase(density_blocks, False)

        for copy in pos_copies[:4]:
            copy.wait_recv()
        source_features(pos_cor[par, 0], pos_cor[par, 1], jfh, 2, 8)
        for srow in (0, rows + 1):
            build_lhs(srow, 0)
        outer_phase(density_blocks, True)

        best = [jnp.full((width, slots), -SENTINEL, jnp.float32)] * 4
        for row in range(rows):
            for p in range(half):
                got = jnp.sum(dsum[row, p], axis=0, keepdims=True)
                dens[row, p + 1 : p + 2, :] = got[:, :slots]
                dens[row, cols - p : cols - p + 1, :] = got[:, slots:]
        for row in range(rows):
            code = base[6, row]
            live = code > 0.5
            heavy = code > 1.5
            density = KERNEL_NORM * dens[row]
            own = density / jnp.where(heavy, REST_HEAVY, REST_LIGHT)
            ratio[row] = own
            light_sel = live & jnp.logical_not(heavy)
            heavy_sel = live & heavy
            for k, (sel, value) in enumerate(
                ((light_sel, own), (heavy_sel, own), (light_sel, -own), (heavy_sel, -own))
            ):
                best[k] = jnp.maximum(best[k], jnp.where(sel, value, -SENTINEL))
        lane = lax.broadcasted_iota(jnp.int32, (1, slots), 1)
        mine = jnp.full((1, slots), -SENTINEL, jnp.float32)
        for k in range(4):
            peak = jnp.max(jnp.max(best[k], axis=0, keepdims=True), axis=1, keepdims=True)
            mine = jnp.where(lane == k, peak, mine)
        red_snd[par] = mine
        for k, (dx, dy) in enumerate(peers):
            remote(
                red_snd.at[par],
                red_rcv.at[par, pl.ds(k, 1)],
                red_ss.at[par],
                red_rs.at[par],
                at_x(dx),
                at_y(dy),
            ).start()

        for row in range(rows):
            code = base[6, row]
            live = code > 0.5
            heavy = code > 1.5
            own = ratio[row]
            density = KERNEL_NORM * dens[row]
            safe = jnp.where(live, density, 1.0)
            scale = 1.0 / (safe * safe)
            stiff = jnp.where(heavy, STIFF_HEAVY, STIFF_LIGHT)
            beta = jnp.where(live, stiff * (own - 1.0) * scale, 0.0)
            parts[0, row] = jnp.where(live, press[row] * scale, 0.0)
            parts[1, row] = jnp.where(heavy, 0.0, beta)
            parts[2, row] = jnp.where(heavy, beta, 0.0)
        pack_columns(parts, ab_pack, 3)
        ab_copies = halo(parts, ab_pack, ab_row, ab_col, ab_cor, ab_ss, ab_rs, par)
        for copy in ab_copies:
            copy.start()

        for row in range(rows):
            value_rows(
                pos[0, row], pos[1, row], [parts[k, row] for k in range(3)], vf, row + 1, width
            )
        inner_phase(force_blocks)

        for copy in ab_copies[4:]:
            copy.wait_recv()
        for side, srow in enumerate((0, rows + 1)):
            value_rows(
                pos_row[par, side, 0], pos_row[par, side, 1],
                [ab_row[par, side, k] for k in range(3)], vf, srow, width,
            )
            value_rows(
                pos_col[par, side, 0], pos_col[par, side, 1],
                [ab_col[par, side, k] for k in range(3)], vfh, side, 8,
            )
        outer_phase(force_blocks, False)
        for copy in ab_copies[:4]:
            copy.wait_recv()
        value_rows(
            pos_cor[par, 0], pos_cor[par, 1], [ab_cor[par, k] for k in range(3)], vfh, 2, 8
        )
        outer_phase(force_blocks, True)

        for copy in pos_copies + ab_copies:
            copy.wait_send()
        everyone = red_rcv.at[par, pl.ds(0, others)]
        pltpu.make_async_copy(everyone, everyone, red_ss.at[par]).wait()
        pltpu.make_async_copy(everyone, everyone, red_rs.at[par]).wait()
        top = jnp.maximum(
            red_snd[par], jnp.max(red_rcv[par, 0:others, :], axis=0, keepdims=True)
        )
        bound = [
            jnp.max(jnp.where(lane == k, top, -SENTINEL), axis=1, keepdims=True)
            for k in range(4)
        ]
        bounds_out[it] = jnp.where(lane < 2, top, -top)
        relax_light = 1.0 / (1.0 + bound[0] + bound[2])
        relax_heavy = 1.0 / (1.0 + bound[1] + bound[3])

        for row in range(rows):
            def total(k):
                return sums[row, k * width : (k + 1) * width, :]

            def linear(k, mid):
                return (
                    (total(k) + total(k + mid))
                    + relax_light * (total(k + 1) + total(k + 1 + mid))
                    + relax_heavy * (total(k + 2) + total(k + 2 + mid))
                )

            code = base[6, row]
            live = code > 0.5
            heavy = code > 1.5
            relaxed = jnp.where(heavy, STIFF_HEAVY * relax_heavy, STIFF_LIGHT * relax_light)
            press[row] = jnp.where(live, press[row] + relaxed * (ratio[row] - 1.0), 0.0)
            term = parts[0, row] + relax_light * parts[1, row] + relax_heavy * parts[2, row]
            scale = jnp.where(
                heavy, 6.0 * KERNEL_NORM / MASS_HEAVY, 6.0 * KERNEL_NORM / MASS_LIGHT
            )
            plain, by_term = total(0), linear(1, 3)
            for c in range(2):
                own = pos[c, row] - 0.5
                first = 8 + 8 * c
                placed = total(first) + total(first + 4)
                force = term * (own * plain - placed) + own * by_term - linear(first + 1, 4)
                acc[c, row] = jnp.where(live, scale * force, 0.0)
        return carry

    lax.fori_loop(0, ITERS, one_iteration, 0)

    for row in range(rows):
        live = base[6, row] > 0.5
        press_out[row] = press[row, 1 : cols + 1, :]
        for c in range(2):
            vel = base[2 + c, row] + TIME_STEP * (base[4 + c, row] + acc[c, row])
            vel = jnp.where(live, vel, 0.0)
            place = jnp.where(live, base[c, row] + TIME_STEP * vel, 0.0)
            vel_out[c, row] = vel[1 : cols + 1]
            pos_out[c, row] = place[1 : cols + 1]


def local(position, velocity, other_accel, phase_ids, counts):
    rows, cols, slots = phase_ids.shape
    width, half = cols + 2, cols // 2
    nx, ny = lax.axis_size("gx"), lax.axis_size("gy")
    tall = -(-rows // 8) * 8
    slot_index = jnp.arange(slots, dtype=jnp.int32)
    live = slot_index[None, None, :] < counts[:, :, None]
    codes = jnp.where(live, phase_ids + 1, 0).astype(jnp.float32)

    def vm(*shape):
        return pltpu.VMEM(shape, jnp.float32)

    dma = pltpu.SemaphoreType.DMA
    new_pos, new_vel, pressure, bounds = pl.pallas_call(
        functools.partial(step_kernel, nx, ny),
        out_shape=(
            jax.ShapeDtypeStruct((2, rows, cols, slots), jnp.float32),
            jax.ShapeDtypeStruct((2, rows, cols, slots), jnp.float32),
            jax.ShapeDtypeStruct((rows, cols, slots), jnp.float32),
            jax.ShapeDtypeStruct((ITERS, 1, slots), jnp.float32),
        ),
        in_specs=[pl.BlockSpec(memory_space=pltpu.VMEM)] * 4,
        out_specs=(pl.BlockSpec(memory_space=pltpu.VMEM),) * 4,
        scratch_shapes=[
            vm(7, rows, width, slots),
            vm(2, rows, width, slots),
            vm(2, rows, width, slots),
            vm(rows, width, slots),
            vm(3, rows, width, slots),
            vm(rows, width, slots),
            vm(rows, width, slots),
            vm(rows, half, 8, 2 * slots),
            vm(rows + 2, 24 * width, slots),
            vm(3, 24 * tall, slots),
            pltpu.VMEM((rows + 2, half + 2, slots, 48), jnp.bfloat16),
            vm(rows, 3, 8 * width, slots),
            vm(rows, 3, 8 * width, slots),
            vm(rows, 9, 8 * width, slots),
            vm(rows + 2, 56 * width, slots),
            vm(3, 56 * tall, slots),
            vm(rows, 24 * width, slots),
            vm(rows, half, 9, slots, 2 * slots),
            vm(2, 2, tall, slots),
            vm(2, 2, 2, width, slots),
            vm(2, 2, 2, tall, slots),
            vm(2, 2, tall, slots),
            vm(2, 3, tall, slots),
            vm(2, 2, 3, width, slots),
            vm(2, 2, 3, tall, slots),
            vm(2, 3, tall, slots),
            vm(2, 1, slots),
            vm(2, nx * ny, slots),
            dma((2, 8)), dma((2, 8)), dma((2, 8)), dma((2, 8)), dma((2,)), dma((2,)),
        ],
        compiler_params=pltpu.CompilerParams(collective_id=0, has_side_effects=True),
    )(position, velocity, other_accel, codes)
    return new_pos, new_vel, pressure, bounds[:, 0, :4]


def solution(mesh):
    placed = (
        P(None, "gx", "gy", None),
        P(None, "gx", "gy", None),
        P(None, "gx", "gy", None),
        P("gx", "gy", None),
        P("gx", "gy"),
    )
    return jax.shard_map(
        local,
        mesh=mesh,
        in_specs=placed,
        out_specs=(P(None, "gx", "gy", None), P(None, "gx", "gy", None), P("gx", "gy", None), P()),
        check_vma=False,
    )
```

time: 110 us -> 59.8 us (0.54)
  Pallas kernels: 101 us -> 51.6 us
    pallas_call x1, Pallas kernels: 101 us -> 51.6 us  [local(): pl.pallas_call(functools.partial(step_kernel, nx, ny), out_shape=(jax.Sha...]
where the time goes in v1:
time: 59.8 us; the launch traced here: 59.3 us
  Pallas kernels  51.6 us (86%)
  local copies, waits for them, and re-layouts  5.59 us (9%)
  other arithmetic  1.43 us (2%)
  between operations  0.66 us (1%)
    pallas_call x1, Pallas kernels, local(): pl.pallas_call(functools.partial(step_kernel, nx, ny), out_shape=(jax.Sha...  51.6 us
    unnamed x19, local copies, waits for them, and re-layouts  5.59 us
    convert_element_type x1, other arithmetic, local(): codes = jnp.where(live, phase_ids + 1, 0).astype(jnp.float32)  1.43 us

profile of v1, /device:TPU:0, one launch (start us, length us, event | category | flops | bytes accessed | tf_op | source)
XLA Modules:
  0.0 59.3 jit_solution(2624059157423436453)
XLA Ops:
  0.6 0.0 copy-start.1
  0.6 1.4 %select_convert_fusion.code_in = f32[6,6,128]{2,1,0:T(8,128)} fusion(s32[6,6,128]{2,1,0:T(8,128)} %param.8, s32[6,6]{1,0:T(8,128)} %param.9), kind=kLoop, calls=%fused_computation | loop fusion | flops 18432 | bytes 37008 | tf_op jit(solution)/shard_map/convert_element_type | solution.py:496
  2.1 0.0 copy-done.1
  2.1 0.0 copy-start.2
  2.1 0.6 %copy.9.pos_in = f32[2,6,6,128]{3,2,1,0:T(8,128)} copy(f32[2,6,6,128]{3,0,2,1:T(2,128)S(1)} %copy-done.1) | data formatting | bytes 73728 | tf_op args[0]
  2.7 0.1 copy-done.2
  2.8 0.0 copy-start.3
  2.8 0.6 %copy.10.vel_in = f32[2,6,6,128]{3,2,1,0:T(8,128)} copy(f32[2,6,6,128]{3,0,2,1:T(2,128)S(1)} %copy-done.2) | data formatting | bytes 73728 | tf_op args[1]
  3.5 0.1 copy-done.3
  3.6 0.6 %copy.11.oth_in = f32[2,6,6,128]{3,2,1,0:T(8,128)} copy(f32[2,6,6,128]{3,0,2,1:T(2,128)S(1)} %copy-done.3) | data formatting | bytes 73728 | tf_op args[2]
  4.2 51.6 %shard_map.84 = (f32[2,6,6,128]{3,2,1,0:T(8,128)}, f32[2,6,6,128]{3,2,1,0:T(8,128)}, f32[6,6,128]{2,1,0:T(8,128)}, f32[4,1,128]{2,1,0:T(1,128)}) custom-call(f32[2,6,6,128]{3,2,1,0:T(8,128)} %copy.9.pos_in, f32[2,6,6,128]{3,2,1,0:T(8,128)} %copy.10.vel_in, f32[2,6,6,128]{3,2,1,0:T(8,128)} %copy.11.oth_in, f32[6,6,128]{2,1,0:T(8,128)} %select_convert_fusion.code_in), custom_call_target="tpu_custom_call" | custom-call | tf_op jit(solution)/shard_map/pallas_call | solution.py:502
  55.8 0.0 copy-start
  55.9 1.4 %copy.12 = f32[2,6,6,128]{3,0,2,1:T(2,128)} copy(f32[2,6,6,128]{3,2,1,0:T(8,128)} %get-tuple-element.12) | data formatting | bytes 73728
  57.3 0.0 copy-done
  57.3 0.0 copy-start.4
  57.3 0.6 %copy.13 = f32[2,6,6,128]{3,0,2,1:T(2,128)} copy(f32[2,6,6,128]{3,2,1,0:T(8,128)S(1)} %copy-done) | data formatting | bytes 73728
  57.9 0.1 copy-done.4
  58.0 0.0 copy-start.5
  58.0 0.6 %copy.16 = f32[6,6,128]{2,1,0:T(8,128)} copy(f32[6,6,128]{2,1,0:T(8,128)S(1)} %copy-done.4) | data formatting | bytes 36864
  58.7 0.1 copy-done.5
  58.7 0.6 copy.17
Async XLA Ops:
  0.6 1.4 %copy-start.1 = (f32[2,6,6,128]{3,0,2,1:T(2,128)S(1)}, f32[2,6,6,128]{3,0,2,1:T(2,128)}, u32[]{:S(2)}) copy-start(f32[2,6,6,128]{3,0,2,1:T(2,128)} %param.5) | copy-start | bytes 110596
  2.1 0.8 %copy-start.2 = (f32[2,6,6,128]{3,0,2,1:T(2,128)S(1)}, f32[2,6,6,128]{3,0,2,1:T(2,128)}, u32[]{:S(2)}) copy-start(f32[2,6,6,128]{3,0,2,1:T(2,128)} %param.6) | copy-start | bytes 110596
  2.8 0.8 %copy-start.3 = (f32[2,6,6,128]{3,0,2,1:T(2,128)S(1)}, f32[2,6,6,128]{3,0,2,1:T(2,128)}, u32[]{:S(2)}) copy-start(f32[2,6,6,128]{3,0,2,1:T(2,128)} %param.7) | copy-start | bytes 110596
  55.8 1.5 %copy-start = (f32[2,6,6,128]{3,2,1,0:T(8,128)S(1)}, f32[2,6,6,128]{3,2,1,0:T(8,128)}, u32[]{:S(2)}) copy-start(f32[2,6,6,128]{3,2,1,0:T(8,128)} %get-tuple-element.13) | copy-start | bytes 110596
  57.3 0.7 %copy-start.4 = (f32[6,6,128]{2,1,0:T(8,128)S(1)}, f32[6,6,128]{2,1,0:T(8,128)}, u32[]{:S(2)}) copy-start(f32[6,6,128]{2,1,0:T(8,128)} %get-tuple-element.22) | copy-start | bytes 55300
  58.0 0.7 %copy-start.5 = (f32[4,1,128]{2,1,0:T(1,128)S(1)}, f32[4,1,128]{2,1,0:T(1,128)}, u32[]{:S(2)}) copy-start(f32[4,1,128]{2,1,0:T(1,128)} %get-tuple-element.11) | copy-start | bytes 6148

commit v2 on v1

--- a/solution.py
+++ b/solution.py
@@ -127,15 +127,16 @@
 
 def step_kernel(
     nx, ny,
-    pos_in, vel_in, oth_in, code_in,
+    pos_in, vel_in, oth_in, phase_in, counts_in,
     pos_out, vel_out, press_out, bounds_out,
+    phases, counts, in_sem,
     base, pos, acc, press, parts, ratio, dens, dsum,
     jf, jfh, lhs, xf, yf, af, vf, vfh, sums, gram,
     pos_pack, pos_row, pos_col, pos_cor, ab_pack, ab_row, ab_col, ab_cor,
     red_snd, red_rcv,
     pos_ss, pos_rs, ab_ss, ab_rs, red_ss, red_rs,
 ):
-    _, rows, cols, slots = pos_in.shape
+    rows, cols, _, slots = pos_in.shape
     width, half = cols + 2, cols // 2
     others = nx * ny - 1
     me_x, me_y = lax.axis_index("gx"), lax.axis_index("gy")
@@ -146,6 +147,25 @@
     def at_y(step):
         return lax.rem(me_y + step + ny, ny)
 
+    for k in range(6):
+        for row in range(rows):
+            for cell in (0, width - 1):
+                base[k, row, cell : cell + 1, :] = jnp.zeros((1, slots), jnp.float32)
+    loads = [
+        pltpu.make_async_copy(phase_in, phases, in_sem.at[6]),
+        pltpu.make_async_copy(counts_in, counts, in_sem.at[7]),
+    ]
+    for k, source in enumerate((pos_in, vel_in, oth_in)):
+        for c in range(2):
+            loads.append(
+                pltpu.make_async_copy(
+                    source.at[:, :, c],
+                    base.at[2 * k + c, :, pl.ds(1, cols)],
+                    in_sem.at[2 * k + c],
+                )
+            )
+    for copy in loads:
+        copy.start()
     for ref in (pos_row, pos_col, pos_cor, ab_row, ab_col, ab_cor):
         ref[...] = jnp.zeros_like(ref)
     peers = [(dx, dy) for dx in range(nx) for dy in range(ny) if dx or dy]
@@ -155,19 +175,23 @@
             barrier, inc=1, device_id=(at_x(dx), at_y(dy)), device_id_type=pl.DeviceIdType.MESH
         )
 
-    for ref in (base, acc, press, pos, dens, ratio, parts, sums, pos_pack, ab_pack):
+    for ref in (acc, press, pos, dens, ratio, parts, sums, pos_pack, ab_pack):
         ref[...] = jnp.zeros_like(ref)
     like = jnp.zeros((width, slots), jnp.float32)
     for row in range(rows):
-        for k, source in enumerate((pos_in, vel_in, oth_in)):
-            for c in range(2):
-                base[2 * k + c, row, 1 : cols + 1, :] = source[c, row]
-        base[6, row, 1 : cols + 1, :] = code_in[row]
+        base[6, row] = like
         target_constants(xf, yf, af, row, width, like)
     for row in range(rows + 2):
         source_constants(jf, row, width, like)
     for at in range(3):
         source_constants(jfh, at, 8, jnp.zeros((8, slots), jnp.float32))
+    for copy in loads:
+        copy.wait()
+    slot = lax.broadcasted_iota(jnp.int32, (1, slots), 1)
+    for row in range(rows):
+        for cell in range(cols):
+            code = jnp.where(slot < counts[row, cell], phases[row, cell : cell + 1, :] + 1, 0)
+            base[6, row, cell + 1 : cell + 2, :] = code.astype(jnp.float32)
     pl.semaphore_wait(barrier, others)
 
     def halo(field, pack, row_got, col_got, cor_got, send, recv, par):
@@ -252,7 +276,7 @@
         ]
 
     def force_blocks(row, p, blocks, fresh):
-        left, high, low = [], [], []
+        left, both = [], []
         for ax, ay in blocks:
             q = p + ay
             left.append(
@@ -264,11 +288,12 @@
             )
             g = gram[row, p, 3 * ax + ay]
             h = g.astype(jnp.bfloat16)
-            high.append(h)
-            low.append((g - h.astype(jnp.float32)).astype(jnp.bfloat16))
+            left.append(left[-1])
+            both.append(h)
+            both.append((g - h.astype(jnp.float32)).astype(jnp.bfloat16))
         got = jnp.dot(
-            jnp.concatenate(left + left, axis=1),
-            jnp.concatenate(high + low, axis=0),
+            jnp.concatenate(left, axis=1),
+            jnp.concatenate(both, axis=0),
             preferred_element_type=jnp.float32,
         )
         for col, piece in ((p + 1, got[:24, :slots]), (cols - p, got[24:, slots:])):
@@ -477,13 +502,41 @@
 
     for row in range(rows):
         live = base[6, row] > 0.5
-        press_out[row] = press[row, 1 : cols + 1, :]
+        press_out[row] = press[row]
         for c in range(2):
             vel = base[2 + c, row] + TIME_STEP * (base[4 + c, row] + acc[c, row])
             vel = jnp.where(live, vel, 0.0)
-            place = jnp.where(live, base[c, row] + TIME_STEP * vel, 0.0)
-            vel_out[c, row] = vel[1 : cols + 1]
-            pos_out[c, row] = place[1 : cols + 1]
+            vel_out[c, row] = vel
+            pos_out[c, row] = jnp.where(live, base[c, row] + TIME_STEP * vel, 0.0)
+
+
+def deliver_kernel(
+    pos_in, vel_in, press_in, bounds_in, pos_out, vel_out, press_out, bounds_out, sem
+):
+    cols = press_out.shape[1]
+    stores = [
+        (press_in.at[:, pl.ds(1, cols)], press_out),
+        (bounds_in, bounds_out),
+    ]
+    for source, target in ((pos_in, pos_out), (vel_in, vel_out)):
+        for c in range(2):
+            stores.append((source.at[c, :, pl.ds(1, cols)], target.at[:, :, c]))
+    copies = [
+        pltpu.make_async_copy(source, target, sem.at[k])
+        for k, (source, target) in enumerate(stores)
+    ]
+    for copy in copies:
+        copy.start()
+    for copy in copies:
+        copy.wait()
+
+
+def cell_major(field):
+    return jnp.transpose(field, (1, 2, 0, 3))
+
+
+def slot_major(field):
+    return jnp.transpose(field, (2, 0, 1, 3))
 
 
 def local(position, velocity, other_accel, phase_ids, counts):
@@ -491,25 +544,24 @@
     width, half = cols + 2, cols // 2
     nx, ny = lax.axis_size("gx"), lax.axis_size("gy")
     tall = -(-rows // 8) * 8
-    slot_index = jnp.arange(slots, dtype=jnp.int32)
-    live = slot_index[None, None, :] < counts[:, :, None]
-    codes = jnp.where(live, phase_ids + 1, 0).astype(jnp.float32)
-
     def vm(*shape):
         return pltpu.VMEM(shape, jnp.float32)
 
     dma = pltpu.SemaphoreType.DMA
-    new_pos, new_vel, pressure, bounds = pl.pallas_call(
+    held = pl.pallas_call(
         functools.partial(step_kernel, nx, ny),
         out_shape=(
-            jax.ShapeDtypeStruct((2, rows, cols, slots), jnp.float32),
-            jax.ShapeDtypeStruct((2, rows, cols, slots), jnp.float32),
-            jax.ShapeDtypeStruct((rows, cols, slots), jnp.float32),
-            jax.ShapeDtypeStruct((ITERS, 1, slots), jnp.float32),
+            pltpu.VMEM((2, rows, width, slots), jnp.float32),
+            pltpu.VMEM((2, rows, width, slots), jnp.float32),
+            pltpu.VMEM((rows, width, slots), jnp.float32),
+            pltpu.VMEM((ITERS, 1, slots), jnp.float32),
         ),
-        in_specs=[pl.BlockSpec(memory_space=pltpu.VMEM)] * 4,
+        in_specs=[pl.BlockSpec(memory_space=pltpu.HBM)] * 5,
         out_specs=(pl.BlockSpec(memory_space=pltpu.VMEM),) * 4,
         scratch_shapes=[
+            pltpu.VMEM((rows, cols, slots), jnp.int32),
+            pltpu.SMEM((rows, cols), jnp.int32),
+            dma((8,)),
             vm(7, rows, width, slots),
             vm(2, rows, width, slots),
             vm(2, rows, width, slots),
@@ -540,9 +592,22 @@
             vm(2, nx * ny, slots),
             dma((2, 8)), dma((2, 8)), dma((2, 8)), dma((2, 8)), dma((2,)), dma((2,)),
         ],
-        compiler_params=pltpu.CompilerParams(collective_id=0, has_side_effects=True),
-    )(position, velocity, other_accel, codes)
-    return new_pos, new_vel, pressure, bounds[:, 0, :4]
+        compiler_params=pltpu.CompilerParams(collective_id=0, has_side_effects=True, vmem_limit_bytes=40 * 2**20),
+    )(*[pltpu.with_memory_space_constraint(v, pltpu.HBM) for v in (cell_major(position), cell_major(velocity), cell_major(other_accel), phase_ids, counts)])
+    new_pos, new_vel, pressure, bounds = pl.pallas_call(
+        deliver_kernel,
+        out_shape=(
+            jax.ShapeDtypeStruct((rows, cols, 2, slots), jnp.float32),
+            jax.ShapeDtypeStruct((rows, cols, 2, slots), jnp.float32),
+            jax.ShapeDtypeStruct((rows, cols, slots), jnp.float32),
+            jax.ShapeDtypeStruct((ITERS, 1, slots), jnp.float32),
+        ),
+        in_specs=[pl.BlockSpec(memory_space=pl.ANY)] * 4,
+        out_specs=(pl.BlockSpec(memory_space=pl.ANY),) * 4,
+        scratch_shapes=[dma((6,))],
+        compiler_params=pltpu.CompilerParams(vmem_limit_bytes=2**20),
+    )(*held)
+    return slot_major(new_pos), slot_major(new_vel), pressure, bounds[:, 0, :4]
 
 
 def solution(mesh):

time: 59.8 us -> 47.8 us (0.80)
  local copies, waits for them, and re-layouts: 5.59 us -> 0 us
  Pallas kernels: 51.6 us -> 47 us
  other arithmetic: 1.43 us -> 0 us
    unnamed x19 -> x0, local copies, waits for them, and re-layouts: 5.59 us -> none
    pallas_call x1 -> x2, Pallas kernels: 51.6 us -> 47 us  [the longest x1 46.3 us: local(): pl.pallas_call(functools.partial(step_kernel, nx, ny), out_shape=(pltpu.V...]
    convert_element_type x1 -> x0, other arithmetic: 1.43 us -> none  [local(): codes = jnp.where(live, phase_ids + 1, 0).astype(jnp.float32)]
where the time goes in v2:
time: 47.8 us; the launch traced here: 47.6 us
  Pallas kernels  47 us (98%)
  between operations  0.64 us (1%)
    pallas_call x1, Pallas kernels, local(): pl.pallas_call(functools.partial(step_kernel, nx, ny), out_shape=(pltpu.V...  46.3 us

profile of v2, /device:TPU:0, one launch (start us, length us, event | category | flops | bytes accessed | tf_op | source)
XLA Modules:
  0.0 47.6 jit_solution(343811713929660729)
XLA Ops:
  0.6 46.3 %shard_map.84 = (f32[2,6,8,128]{3,2,1,0:T(8,128)S(1)}, f32[2,6,8,128]{3,2,1,0:T(8,128)S(1)}, f32[6,8,128]{2,1,0:T(8,128)S(1)}, f32[4,1,128]{2,1,0:T(1,128)S(1)}) custom-call(f32[6,6,2,128]{3,2,1,0:T(2,128)} %bitcast.7, f32[6,6,2,128]{3,2,1,0:T(2,128)} %bitcast.8, f32[6,6,2,128]{3,2,1,0:T(2,128)} %bitcast.9, s32[6,6,128]{2,1,0:T(8,128)} %phase_in.1, ...), custom_call_target="tpu_custom_call" | custom-call | tf_op jit(solution)/shard_map/pallas_call | solution.py:551
  46.9 0.7 %shard_map.85 = (f32[6,6,2,128]{3,2,1,0:T(2,128)}, f32[6,6,2,128]{3,2,1,0:T(2,128)}, f32[6,6,128]{2,1,0:T(8,128)}, f32[4,1,128]{2,1,0:T(1,128)}) custom-call(f32[2,6,8,128]{3,2,1,0:T(8,128)S(1)} %get-tuple-element.12.pos_in, f32[2,6,8,128]{3,2,1,0:T(8,128)S(1)} %get-tuple-element.13.vel_in, f32[6,8,128]{2,1,0:T(8,128)S(1)} %get-tuple-element.14.press_in, ...), custom_call_target="tpu_custom_call" | custom-call | tf_op jit(solution)/shard_map/pallas_call | solution.py:597

commit v3 on v2

--- a/solution.py
+++ b/solution.py
@@ -141,11 +141,24 @@
     others = nx * ny - 1
     me_x, me_y = lax.axis_index("gx"), lax.axis_index("gy")
 
+    def wrapped(at, size):
+        at = jnp.where(at < 0, at + size, at)
+        return jnp.where(at >= size, at - size, at)
+
     def at_x(step):
-        return lax.rem(me_x + step + nx, nx)
+        return wrapped(me_x + step, nx)
 
     def at_y(step):
-        return lax.rem(me_y + step + ny, ny)
+        return wrapped(me_y + step, ny)
+
+    for ref in (pos_row, pos_col, pos_cor, ab_row, ab_col, ab_cor):
+        ref[...] = jnp.zeros_like(ref)
+    peers = [(dx, dy) for dx in range(nx) for dy in range(ny) if dx or dy]
+    barrier = pltpu.get_barrier_semaphore()
+    for dx, dy in peers:
+        pl.semaphore_signal(
+            barrier, inc=1, device_id=(at_x(dx), at_y(dy)), device_id_type=pl.DeviceIdType.MESH
+        )
 
     for k in range(6):
         for row in range(rows):
@@ -166,15 +179,6 @@
             )
     for copy in loads:
         copy.start()
-    for ref in (pos_row, pos_col, pos_cor, ab_row, ab_col, ab_cor):
-        ref[...] = jnp.zeros_like(ref)
-    peers = [(dx, dy) for dx in range(nx) for dy in range(ny) if dx or dy]
-    barrier = pltpu.get_barrier_semaphore()
-    for dx, dy in peers:
-        pl.semaphore_signal(
-            barrier, inc=1, device_id=(at_x(dx), at_y(dy)), device_id_type=pl.DeviceIdType.MESH
-        )
-
     for ref in (acc, press, pos, dens, ratio, parts, sums, pos_pack, ab_pack):
         ref[...] = jnp.zeros_like(ref)
     like = jnp.zeros((width, slots), jnp.float32)
@@ -309,15 +313,16 @@
             if 1 <= row + ax <= rows and 1 <= p + ay <= cols
         ]
 
-    def inner_phase(blocks_of):
+    def inner_phase(blocks_of, unrolled=False):
         def middle(step, carry):
             for k in range(2):
                 for p in range(half):
                     blocks_of(1 + 2 * step + k, p, inner_blocks(1, p), True)
             return carry
 
-        pairs = (rows - 2) // 2
-        lax.fori_loop(0, pairs, middle, 0)
+        pairs = 0 if unrolled else (rows - 2) // 2
+        if pairs:
+            lax.fori_loop(0, pairs, middle, 0)
         for row in [0] + list(range(1 + 2 * pairs, rows)):
             for p in range(half):
                 blocks_of(row, p, inner_blocks(row, p), True)
@@ -335,6 +340,30 @@
                 if blocks:
                     blocks_of(row, p, blocks, False)
 
+    def settle(row, p):
+        got = jnp.sum(dsum[row, p], axis=0, keepdims=True)
+        dens[row, p + 1 : p + 2, :] = got[:, :slots]
+        dens[row, cols - p : cols - p + 1, :] = got[:, slots:]
+
+    def ratio_row(row, best):
+        code = base[6, row]
+        live = code > 0.5
+        heavy = code > 1.5
+        own = KERNEL_NORM * dens[row] / jnp.where(heavy, REST_HEAVY, REST_LIGHT)
+        ratio[row] = own
+        light_sel = live & jnp.logical_not(heavy)
+        heavy_sel = live & heavy
+        picks = ((light_sel, own), (heavy_sel, own), (light_sel, -own), (heavy_sel, -own))
+        return [
+            jnp.maximum(old, jnp.where(sel, value, -SENTINEL))
+            for old, (sel, value) in zip(best, picks)
+        ]
+
+    def bounds_row(row, best):
+        for p in range(half):
+            settle(row, p)
+        return ratio_row(row, best)
+
     def one_iteration(it, carry):
         par = lax.rem(it, 2)
 
@@ -355,7 +384,7 @@
                 build_lhs(row + 1, q)
         for row in range(rows):
             target_features(pos[0, row], pos[1, row], xf, yf, af, row, width)
-        inner_phase(density_blocks)
+        inner_phase(density_blocks, True)
 
         for copy in pos_copies[4:]:
             copy.wait_recv()
@@ -368,32 +397,23 @@
             build_lhs(row + 1, 0)
         outer_phase(density_blocks, False)
 
+        best = [jnp.full((width, slots), -SENTINEL, jnp.float32)] * 4
+        late = [row for row in range(rows) if row in (0, rows - 1)]
+        early = [row for row in range(rows) if row not in late]
+        for row in early:
+            best = bounds_row(row, best)
+        for row in late:
+            for p in range(1, half):
+                settle(row, p)
         for copy in pos_copies[:4]:
             copy.wait_recv()
         source_features(pos_cor[par, 0], pos_cor[par, 1], jfh, 2, 8)
         for srow in (0, rows + 1):
             build_lhs(srow, 0)
         outer_phase(density_blocks, True)
-
-        best = [jnp.full((width, slots), -SENTINEL, jnp.float32)] * 4
-        for row in range(rows):
-            for p in range(half):
-                got = jnp.sum(dsum[row, p], axis=0, keepdims=True)
-                dens[row, p + 1 : p + 2, :] = got[:, :slots]
-                dens[row, cols - p : cols - p + 1, :] = got[:, slots:]
-        for row in range(rows):
-            code = base[6, row]
-            live = code > 0.5
-            heavy = code > 1.5
-            density = KERNEL_NORM * dens[row]
-            own = density / jnp.where(heavy, REST_HEAVY, REST_LIGHT)
-            ratio[row] = own
-            light_sel = live & jnp.logical_not(heavy)
-            heavy_sel = live & heavy
-            for k, (sel, value) in enumerate(
-                ((light_sel, own), (heavy_sel, own), (light_sel, -own), (heavy_sel, -own))
-            ):
-                best[k] = jnp.maximum(best[k], jnp.where(sel, value, -SENTINEL))
+        for row in late:
+            settle(row, 0)
+            best = ratio_row(row, best)
         lane = lax.broadcasted_iota(jnp.int32, (1, slots), 1)
         mine = jnp.full((1, slots), -SENTINEL, jnp.float32)
         for k in range(4):
@@ -432,7 +452,7 @@
             value_rows(
                 pos[0, row], pos[1, row], [parts[k, row] for k in range(3)], vf, row + 1, width
             )
-        inner_phase(force_blocks)
+        inner_phase(force_blocks, True)
 
         for copy in ab_copies[4:]:
             copy.wait_recv()

time: 47.8 us -> 47.5 us (level)
  no operation moved by 1% of the time
where the time goes in v3:
time: 47.5 us; the launch traced here: 47.3 us
  Pallas kernels  46.7 us (98%)
  between operations  0.64 us (1%)
    pallas_call x1, Pallas kernels, local(): pl.pallas_call(functools.partial(step_kernel, nx, ny), out_shape=(pltpu.V...  46 us

profile of v3, /device:TPU:0, one launch (start us, length us, event | category | flops | bytes accessed | tf_op | source)
XLA Modules:
  0.0 47.3 jit_solution(3363898262251737204)
XLA Ops:
  0.6 46.0 %shard_map.84 = (f32[2,6,8,128]{3,2,1,0:T(8,128)S(1)}, f32[2,6,8,128]{3,2,1,0:T(8,128)S(1)}, f32[6,8,128]{2,1,0:T(8,128)S(1)}, f32[4,1,128]{2,1,0:T(1,128)S(1)}) custom-call(f32[6,6,2,128]{3,2,1,0:T(2,128)} %bitcast.7, f32[6,6,2,128]{3,2,1,0:T(2,128)} %bitcast.8, f32[6,6,2,128]{3,2,1,0:T(2,128)} %bitcast.9, s32[6,6,128]{2,1,0:T(8,128)} %phase_in.1, ...), custom_call_target="tpu_custom_call" | custom-call | tf_op jit(solution)/shard_map/pallas_call | solution.py:571
  46.6 0.7 %shard_map.85 = (f32[6,6,2,128]{3,2,1,0:T(2,128)}, f32[6,6,2,128]{3,2,1,0:T(2,128)}, f32[6,6,128]{2,1,0:T(8,128)}, f32[4,1,128]{2,1,0:T(1,128)}) custom-call(f32[2,6,8,128]{3,2,1,0:T(8,128)S(1)} %get-tuple-element.12.pos_in, f32[2,6,8,128]{3,2,1,0:T(8,128)S(1)} %get-tuple-element.13.vel_in, f32[6,8,128]{2,1,0:T(8,128)S(1)} %get-tuple-element.14.press_in, ...), custom_call_target="tpu_custom_call" | custom-call | tf_op jit(solution)/shard_map/pallas_call | solution.py:617
